TPU v7x, 32 devices: a whole 2x2x4 slice. The times are simulated.
32 devices in a mesh: gx: 8 (over y, x, core), gy: 4 (over z).
Axes of the slice: x: 2, y: 2, z: 4, core: 2. Of those that a mesh axis runs over, the one named last changes fastest.
Arguments:
- spectrum: float32 [192, 160, 1080], P('gx', 'gy'), may hold values from 0.05 to 1
- adjoint_in: float32 [192, 160, 1080], P('gx', 'gy'), may hold values from 0 to 2
- current_x: float32 [192, 160], P('gx', 'gy'), may hold values from -0.08 to 0.08
- current_y: float32 [192, 160], P('gx', 'gy'), may hold values from -0.08 to 0.08
- wind_x: float32 [192, 160], P('gx', 'gy'), may hold values from -4 to 4
- wind_y: float32 [192, 160], P('gx', 'gy'), may hold values from -4 to 4
- land_mask: int32 [192, 160], P('gx', 'gy'), may hold values from 0 to 1, as said below
- ice_mask: int32 [192, 160], P('gx', 'gy'), may hold values from 0 to 1, as said below
- group_speed: float32 [30], replicated, may hold values from 0.1 to 0.4
- growth_rate: float32 [30], replicated, may hold values from 0.1 to 1
- dissipation: float32 [30], replicated, may hold values from 0.3 to 3
Outputs:
- adjoint_spectrum: float32 [192, 160, 1080], P('gx', 'gy')
Inputs may be any that keep to these rules, and one draw needn't show every extreme that they name: `land_mask`: 1 marks land, 0 sea. `ice_mask`: 1 marks sea ice, 0 open water.
All inputs are finite; a program needn't handle non-finite values.
Results may differ from a plain program's by a relative error of at most 0.0001.
Values sent between devices are 32-bit elements; how exact they have to be, the bound alone decides.
A program may use at most 128 MiB of HBM per device.

v0:
```python
import functools
import math
from types import SimpleNamespace

import jax
import jax.numpy as jnp
import numpy as np
from jax import lax
from jax.experimental import pallas as pl
from jax.experimental.pallas import tpu as pltpu
from jax.sharding import PartitionSpec as P

DIRS = 36
LANES = 128
TILE = 8
CERTAIN = 0.81
HBM = pl.BlockSpec(memory_space=pltpu.HBM)
VMEM = pl.BlockSpec(memory_space=pltpu.VMEM)
MESH = pl.DeviceIdType.MESH


def lane_chunks(bins):
    return [(c, s, min(LANES, bins - s)) for c, s in enumerate(range(0, bins, LANES))]


def slot_plan(need):
    parts = []
    for c, s, w in lane_chunks(len(need)):
        lane = 0
        while lane < w:
            if not need[s + lane]:
                lane += 1
                continue
            first = lane
            while lane < w and need[s + lane]:
                lane += 1
            parts.append((c, first, lane, w))
    parts.sort(key=lambda p: (p[3] == LANES, p[1] - p[2]))
    slots, used = [], []
    for c, first, last, w in parts:
        size = last - first
        for n, busy in enumerate(used):
            if not busy[first:last].any():
                shift = 0
            elif w == LANES:
                starts = [k for k in range(LANES - size + 1) if not busy[k : k + size].any()]
                if not starts:
                    continue
                shift = starts[0] - first
            else:
                continue
            busy[first + shift : last + shift] = True
            slots[n].append((c, first, last, shift % LANES))
            break
        else:
            busy = np.zeros(LANES, bool)
            busy[first:last] = True
            used.append(busy)
            slots.append([(c, first, last, 0)])
    return slots


def repeat(value, count):
    return value if count == 1 else jnp.concatenate([value] * count, axis=0)


def between(first, last):
    lane = lax.broadcasted_iota(jnp.int32, (TILE, LANES), 1)
    return jnp.logical_and(lane >= first, lane < last)


def pack(plan, chunks, load, out):
    for n, parts in enumerate(plan):
        value, late = None, None
        for c, first, last, shift in parts:
            w = chunks[c][2]
            if w < LANES:
                late = (c, w)
                continue
            part = load(c)
            if shift:
                part = pltpu.roll(part, shift, axis=1)
            begin = (first + shift) % LANES
            value = part if value is None else jnp.where(between(begin, begin + last - first), part, value)
        if value is not None:
            out[n] = value
        if late is not None:
            out[n, :, 0 : late[1]] = load(late[0])


def unpack(plan, chunk, slots):
    c, _, w = chunk
    value = jnp.zeros((TILE, w), jnp.float32)
    for n, parts in enumerate(plan):
        for chunk_of, first, last, shift in parts:
            if chunk_of != c:
                continue
            if w < LANES:
                part = slots[n, :, 0:w]
                if last - first < w:
                    part = jnp.where(between(first, last)[:, 0:w], part, 0.0)
                value = part
                continue
            part = slots[n]
            if shift:
                part = pltpu.roll(part, LANES - shift, axis=1)
            value = part if last - first == LANES else jnp.where(between(first, last), part, value)
    return value


def split3(value):
    high = value.astype(jnp.bfloat16).astype(jnp.float32)
    rest = value - high
    mid = rest.astype(jnp.bfloat16).astype(jnp.float32)
    return [high, mid, rest - mid]


def kernel(
    nx, ny, plan_pos, plan_neg, lat_groups,
    spectrum, adjoint, cx_h, cy_h, wx_h, wy_h, land_h, ice_h, speed_h, growth_h, diss_h, consts_h,
    done,
    both, lat, rim, tt, cxs, fxs, cys, tab, opx, odx, opy, ody, wxs, wys, seas,
    send_s, recv_s, send_t, recv_t, mine_f, mine_i, near_f, near_i, face_f, face_i, coeffs, consts, params, ext, bufs, load_sem, send_sem, recv_sem,
):
    gx, gy = lax.axis_index("gx"), lax.axis_index("gy")
    rows, cells, bins = adjoint.shape
    east, west = lax.rem(gx + 1, nx), lax.rem(gx + nx - 1, nx)
    has_north, has_south = gy < ny - 1, gy > 0
    chunks = lane_chunks(bins)
    tiles = cells // TILE
    f32 = jnp.float32
    sp, adj = both.at[0], both.at[1]

    cx, cy, wx, wy = (mine_f.at[m] for m in range(4))
    land, ice = (mine_i.at[m] for m in range(2))
    speed, growth, diss = (coeffs.at[m] for m in range(3))
    pairs = (rows - 2) // 2
    bounds = [1, 4, 10, 16, rows - 1]
    local = lambda src, dst, n: pltpu.make_async_copy(src, dst, load_sem.at[n])
    ends = [local(spectrum.at[r], sp.at[r], 0) for r in (0, rows - 1)]
    small = [
        local(src, dst, n)
        for src, dst, n in (
            (cx_h, cx, 1), (cy_h, cy, 1), (wx_h, wx, 1), (wy_h, wy, 1), (land_h, land, 2), (ice_h, ice, 2),
            (speed_h, speed, 3), (growth_h, growth, 3), (diss_h, diss, 3), (consts_h, consts, 4),
        )
    ]
    rims = [
        local(spectrum.at[:, pl.ds(0, 1), :], rim.at[0], 5),
        local(spectrum.at[:, pl.ds(cells - 1, 1), :], rim.at[1], 5),
    ]
    groups = []
    for n, (a, b) in enumerate(zip(bounds[:-1], bounds[1:])):
        groups.append(
            [local(src.at[pl.ds(a, b - a)], dst.at[pl.ds(a, b - a)], 6 + n) for src, dst in ((spectrum, sp), (adjoint, adj))]
        )
    last_adj = [local(adjoint.at[r], adj.at[r], 6 + len(groups)) for r in (0, rows - 1)]
    for copy in ends + small + rims:
        copy.start()

    barrier = pltpu.get_barrier_semaphore()
    for where in (east, west):
        pl.semaphore_signal(barrier, inc=1, device_id={"gx": where}, device_id_type=MESH)

    @pl.when(has_north)
    def _():
        pl.semaphore_signal(barrier, inc=1, device_id={"gy": gy + 1}, device_id_type=MESH)

    @pl.when(has_south)
    def _():
        pl.semaphore_signal(barrier, inc=1, device_id={"gy": gy - 1}, device_id_type=MESH)

    for group in groups:
        for copy in group:
            copy.start()
    for copy in last_adj:
        copy.start()

    def far(src, dst, out, n, axis, where):
        return pltpu.make_async_remote_copy(
            src_ref=src, dst_ref=dst, send_sem=send_sem.at[out], recv_sem=recv_sem.at[n],
            device_id={axis: where}, device_id_type=MESH,
        )

    def settle(ref, sem):
        pltpu.make_async_copy(ref, ref, sem).wait()

    order = list(range(1, tiles - 1)) + [0, tiles - 1]
    ahead = []
    for m, (src, dst) in enumerate(((cx, face_f), (land, face_i))):
        ahead.append(far(src.at[pl.ds(rows - TILE, TILE)], dst.at[0], m, m, "gx", east))
        ahead.append(far(src.at[pl.ds(0, TILE)], dst.at[1], m, m, "gx", west))
    lon_s, lon_t = (
        [[far(src.at[p, d], dst.at[p, d], 2 + m, 2 + m * tiles + p, "gx", (east, west)[d]) for d in range(2)] for p in range(tiles)]
        for m, (src, dst) in enumerate(((send_s, recv_s), (send_t, recv_t)))
    )
    split = lat_groups[1][0]
    halves = ((0, split), (split, rows))
    spans = [[g] for g in lat_groups] + [[(0, 1), (rows - 1, rows)]]
    lat_all = []
    for d, (where, there, back_there) in enumerate(((gy + 1, has_north, has_south), (gy - 1, has_south, has_north))):
        sem = 2 + 2 * tiles + 7 * d
        away = lambda src, dst, out, n, where=where, d=d, sem=sem: far(src, dst, 4 + 4 * d + out, sem + n, "gy", where)
        own, halo = ((7 + cells, 7), (8, 8 + cells))[d]
        small_lat = [away(cy, near_f.at[d], 0, 0), away(land, near_i.at[d], 1, 1)]
        first = [away(rim.at[1 - d, pl.ds(a, b - a)], lat.at[d, pl.ds(a, b - a)], 2, 2 + n) for n, (a, b) in enumerate(halves)]
        second = [
            [away(tt.at[pl.ds(a, b - a), :, pl.ds(own, 1)], tt.at[pl.ds(a, b - a), :, pl.ds(halo, 1)], 3, 4 + n) for a, b in span]
            for n, span in enumerate(spans)
        ]
        lat_all.append(SimpleNamespace(
            there=there, back_there=back_there, small=small_lat, first=first, second=second, sem=sem, out=4 + 4 * d, own=own, halo=halo,
        ))

    def lat_start(pick):
        for side in lat_all:
            @pl.when(side.there)
            def _(side=side):
                for copy in pick(side):
                    copy.start()

    def lat_arrive(pick):
        for side in lat_all:
            @pl.when(side.back_there)
            def _(side=side):
                pick(side)

    def first_arrives(n):
        lat_arrive(lambda side: side.first[n].wait_recv())

    def second_arrives(n):
        count = sum(b - a for a, b in spans[n])
        lat_arrive(lambda side: settle(tt.at[pl.ds(0, count), :, pl.ds(side.halo, 1)], recv_sem.at[side.sem + 4 + n]))

    settle(sp.at[pl.ds(0, 2)], load_sem.at[0])
    for p in range(tiles):
        for d, (row, plan) in enumerate(((rows - 1, plan_pos), (0, plan_neg))):
            load = lambda c, row=row, p=p: sp[row, TILE * p : TILE * p + TILE, chunks[c][1] : chunks[c][1] + chunks[c][2]]
            pack(plan, chunks, load, send_s.at[p, d])
    for n, ref in enumerate((mine_f, mine_i, coeffs, consts, rim)):
        settle(ref, load_sem.at[1 + n])

    freqs = coeffs.shape[2]
    params[...] = jnp.zeros(params.shape, f32)
    for m, ref in enumerate((speed, growth, diss)):
        params[TILE * m : TILE * m + TILE, 0:freqs] = jnp.broadcast_to(ref[...], (TILE, freqs))
    pl.semaphore_wait(barrier, 2 + has_north.astype(jnp.int32) + has_south.astype(jnp.int32))
    for copy in ahead:
        copy.start()
    lat_start(lambda side: side.small)
    for p in order:
        for copy in lon_s[p]:
            copy.start()
    lat_start(lambda side: side.first)

    many = params.shape[1]
    hot = consts[0:many].astype(jnp.bfloat16)
    by_bin = sum(
        jnp.dot(part.astype(jnp.bfloat16), hot, preferred_element_type=f32) for part in split3(params[...])
    )
    cosine, sine = consts[many : many + TILE], consts[many + TILE : many + 2 * TILE]
    for c, s, w in chunks:
        cs = slice(s, s + w)
        tab[0, c, :, 0:w] = by_bin[0:TILE, cs] * cosine[:, cs]
        tab[1, c, :, 0:w] = by_bin[0:TILE, cs] * sine[:, cs]
        tab[2, c, :, 0:w] = by_bin[TILE : 2 * TILE, cs] * cosine[:, cs]
        tab[3, c, :, 0:w] = by_bin[TILE : 2 * TILE, cs] * sine[:, cs]
        tab[4, c, :, 0:w] = by_bin[2 * TILE : 3 * TILE, cs]

    sub = lax.broadcasted_iota(jnp.int32, (LANES, 2 * LANES), 0)
    half = (lax.broadcasted_iota(jnp.int32, (LANES, 2 * LANES), 1) >= LANES).astype(jnp.int32)
    row_of = jnp.where(sub < rows, sub, jnp.where(sub < 2 * rows, sub - rows, jnp.where(sub < 3 * rows, sub - 2 * rows, -2)))
    row_of = row_of - half

    def turned(field):
        stack = split3(field)
        stack.append(jnp.zeros((LANES - 3 * rows, LANES), f32))
        return jnp.concatenate(stack, axis=0).T

    def spread(lhs, count, put):
        lhs = lhs.astype(jnp.bfloat16)
        for n in range(count // 2):
            pick = jnp.where(row_of == 2 * n, 1.0, 0.0).astype(jnp.bfloat16)
            out = jnp.dot(lhs, pick, preferred_element_type=f32)
            put(2 * n, out[:, 0:LANES])
            put(2 * n + 1, out[:, LANES:])

    sea_of = lambda mask: (1 - mask).astype(f32)
    ext[...] = jnp.zeros(ext.shape, f32)
    ice_free = sea_of(ice[...])
    ext[0, 1 : rows + 1, 0:cells] = cx[...]
    ext[1, 1 : rows + 1, 0:cells] = sea_of(land[...])
    ext[2, 0:rows, 0:cells] = cy[...]
    ext[3, 0:rows, 0:cells] = sea_of(land[...])
    ext[8, 0:rows, 0:cells] = wx[...] * ice_free
    ext[9, 0:rows, 0:cells] = wy[...] * ice_free
    lane = lax.broadcasted_iota(jnp.int32, (rows, LANES), 1)
    sea, drift = ext[3, 0:rows], ext[2, 0:rows]
    opened_x = ext[1, 0:rows] * ext[1, 1 : rows + 1]
    ahead_of = lambda value: pltpu.roll(value, LANES - 1, axis=1)
    opened_y = sea * ahead_of(sea)
    fields = [
        opened_x, opened_x * (0.5 * (ext[0, 0:rows] + ext[0, 1 : rows + 1])),
        opened_y, opened_y * (0.5 * (drift + ahead_of(drift))),
        ext[8, 0:rows], ext[9, 0:rows], sea,
    ]
    homes = (opx, odx, opy, ody, wxs, wys, seas)

    def put_all(i, block):
        for k, home in enumerate(homes):
            home[i, 0:cells] = block[k * cells : (k + 1) * cells]

    spread(jnp.concatenate([turned(f)[0:cells] for f in fields], axis=0), rows, put_all)

    @pl.when(jnp.logical_not(has_south))
    def _():
        lat[0] = jnp.zeros(lat.shape[1:], f32)

        def clear(r, carry):
            for c, _, _ in chunks:
                tt[r, c, 7:8] = jnp.zeros((1, LANES), f32)
            return carry

        lax.fori_loop(0, rows, clear, 0)

    @pl.when(jnp.logical_not(has_north))
    def _():
        lat[1] = jnp.zeros(lat.shape[1:], f32)

        def clear(r, carry):
            for c, _, _ in chunks:
                tt[r, c, 8 + cells : 9 + cells] = jnp.zeros((1, LANES), f32)
            return carry

        lax.fori_loop(0, rows, clear, 0)

    def lat_part(buf, r, chunk, lo, hi, own):
        c, s, w = chunk
        count = (hi - lo) // TILE
        sine_row = tab[1, c, :, 0:w]
        buf.near[c, lo:hi, 0:w] = own
        buf.near[c, hi : hi + 1, 0:w] = sp[r, hi : hi + 1, s : s + w] if hi < cells else lat[1, r, :, s : s + w]
        upper = buf.near[c, lo + 1 : hi + 1, 0:w]
        courant = opy[r, lo:hi, 0:w] * repeat(sine_row, count) + ody[r, lo:hi, 0:w]
        cys[r, c, 8 + lo : 8 + hi, 0:w] = courant
        fy = courant * jnp.where(courant > 0, own, upper)
        buf.flux[c, 8 + lo : 8 + hi, 0:w] = fy
        at = lo - 1 if lo else cells
        low = opy[r, at : at + 1, 0:w] * sine_row[0:1] + ody[r, at : at + 1, 0:w]
        below = sp[r, lo - 1 : lo, s : s + w] if lo else lat[0, r, :, s : s + w]
        cys[r, c, 7 + lo : 8 + lo, 0:w] = low
        buf.flux[c, 7 + lo : 8 + lo, 0:w] = low * jnp.where(low > 0, below, own[0:1])
        return fy - buf.flux[c, 7 + lo : 7 + hi, 0:w]

    def lon_speed(f, chunk, lo, hi):
        c, _, w = chunk
        speed = opx[f, lo:hi, 0:w] * repeat(tab[0, c, :, 0:w], (hi - lo) // TILE) + odx[f, lo:hi, 0:w]
        cxs[f, c, lo:hi, 0:w] = speed
        return speed

    def upwind(speed, here, there):
        return speed * jnp.where(speed > 0, here, there)

    def gather(totals, rest):
        value = jnp.sum(totals, axis=1, keepdims=True)
        return value if rest is None else value + rest

    def source(buf, r, segments, sums):
        for n, (lo, hi) in enumerate(segments):
            count = (hi - lo) // TILE
            energy = jnp.broadcast_to(gather(*sums[n]) * (1.0 / bins), (hi - lo, LANES))
            total, rest = jnp.zeros((hi - lo, LANES), f32), None
            for c, s, w in chunks:
                advected = buf.moved[c, lo:hi, 0:w]
                blow = wxs[r, lo:hi, 0:w] * repeat(tab[2, c, :, 0:w], count) + wys[r, lo:hi, 0:w] * repeat(tab[3, c, :, 0:w], count)
                gain = 1.0 + jnp.maximum(blow, 0.0)
                scaled = repeat(tab[4, c, :, 0:w], count) * advected
                damp = 1.0 + energy[:, 0:w] * scaled
                weighted = adj[r, lo:hi, s : s + w] * gain / (damp * damp)
                buf.weight[c, lo:hi, 0:w] = weighted
                term = weighted * scaled * advected
                if w == LANES:
                    total = total + term
                else:
                    rest = jnp.sum(term, axis=1, keepdims=True)
            sums[n] = (total, rest)
        yield
        for n, (lo, hi) in enumerate(segments):
            coupling = jnp.broadcast_to(gather(*sums[n]) * (1.0 / bins), (hi - lo, LANES))
            for c, s, w in chunks:
                tt[r, c, 8 + lo : 8 + hi, 0:w] = seas[r, lo:hi, 0:w] * (buf.weight[c, lo:hi, 0:w] - coupling[:, 0:w])
        yield

    slots = [SimpleNamespace(near=bufs.at[4 * q], flux=bufs.at[4 * q + 1], moved=bufs.at[4 * q + 2], weight=bufs.at[4 * q + 3]) for q in range(2)]

    def run(jobs):
        stages = [source(*job) for job in jobs]
        for _ in range(2):
            for stage in stages:
                next(stage)

    def store_moved(buf, chunk, lo, hi, moved, total, rest):
        c, _, w = chunk
        buf.moved[c, lo:hi, 0:w] = moved
        if w == LANES:
            return total + moved, rest
        return total, jnp.sum(moved, axis=1, keepdims=True)

    def row_pair(r, segments):
        sums = [[(jnp.zeros((hi - lo, LANES), f32), None) for lo, hi in segments] for _ in range(2)]
        for chunk in chunks:
            c, s, w = chunk
            for n, (lo, hi) in enumerate(segments):
                own = [sp[r + q, lo:hi, s : s + w] for q in range(3)]
                flux_west = fxs[0, c, lo:hi, 0:w]
                for q in range(2):
                    flux = upwind(lon_speed(r + q + 1, chunk, lo, hi), own[q], own[q + 1])
                    if q:
                        fxs[0, c, lo:hi, 0:w] = flux
                    moved = own[q] - (flux - flux_west) - lat_part(slots[q], r + q, chunk, lo, hi, own[q])
                    flux_west = flux
                    sums[q][n] = store_moved(slots[q], chunk, lo, hi, moved, *sums[q][n])
        run([(slots[q], r + q, segments, sums[q]) for q in range(2)])

    def edge(p):
        lo, hi = TILE * p, TILE * p + TILE
        sums = [[(jnp.zeros((TILE, LANES), f32), None)] for _ in range(2)]
        for chunk in chunks:
            c, s, w = chunk
            for q, r in enumerate((0, rows - 1)):
                own = sp[r, lo:hi, s : s + w]
                if q == 0:
                    flux_west = upwind(lon_speed(0, chunk, lo, hi), unpack(plan_pos, chunk, recv_s.at[p, 0]), own)
                    flux = fxs[1, c, lo:hi, 0:w]
                else:
                    flux_west = fxs[0, c, lo:hi, 0:w]
                    flux = upwind(lon_speed(rows, chunk, lo, hi), own, unpack(plan_neg, chunk, recv_s.at[p, 1]))
                moved = own - (flux - flux_west) - lat_part(slots[q], r, chunk, lo, hi, own)
                sums[q][0] = store_moved(slots[q], chunk, lo, hi, moved, *sums[q][0])
        run([(slots[q], r, [(lo, hi)], sums[q]) for q, r in enumerate((0, rows - 1))])
        for d, (row, plan) in enumerate(((rows - 1, plan_neg), (0, plan_pos))):
            pack(plan, chunks, lambda c, row=row: tt[row, c, 8 + lo : 8 + hi, 0 : chunks[c][2]], send_t.at[p, d])
        for copy in lon_t[p]:
            copy.start()

    def wait_group(n):
        settle(both.at[:, pl.ds(bounds[n], bounds[n + 1] - bounds[n])], load_sem.at[6 + n])

    wait_group(0)
    for chunk in chunks:
        c, s, w = chunk
        for lo in range(0, cells, TILE):
            flux = upwind(lon_speed(1, chunk, lo, lo + TILE), sp[0, lo : lo + TILE, s : s + w], sp[1, lo : lo + TILE, s : s + w])
            for m in range(2):
                fxs[m, c, lo : lo + TILE, 0:w] = flux

    inner = [(TILE, cells - TILE)]
    outer = [(0, TILE), (cells - TILE, cells)]
    firsts = [next(k for k in range(pairs + 1) if 3 + 2 * k >= b) for b in bounds[1:-1]]

    def inner_pair(k, carry):
        for n, first in enumerate(firsts):
            @pl.when(k == first)
            def _(n=n):
                wait_group(n + 1)

        row_pair(1 + 2 * k, inner)
        return carry

    def outer_pair(k, carry):
        row_pair(1 + 2 * k, outer)
        return carry

    lax.fori_loop(0, pairs, inner_pair, 0)
    for n in range(len(firsts)):
        if firsts[n] >= pairs:
            wait_group(n + 1)

    for m, ref in enumerate((face_f, face_i)):
        settle(ref, recv_sem.at[m])
    lat_arrive(lambda side: [copy.wait_recv() for copy in side.small])
    ext[0, 0:1, 0:cells] = face_f[0, TILE - 1 : TILE]
    ext[0, rows + 1 : rows + 2, 0:cells] = face_f[1, 0:1]
    ext[1, 0:1, 0:cells] = sea_of(face_i[0, TILE - 1 : TILE])
    ext[1, rows + 1 : rows + 2, 0:cells] = sea_of(face_i[1, 0:1])
    ext[4, 0:rows, 0:cells] = near_f[0]
    ext[5, 0:rows, 0:cells] = sea_of(near_i[0])
    ext[6, 0:rows, 0:cells] = near_f[1]
    ext[7, 0:rows, 0:cells] = sea_of(near_i[1])
    for n, f in enumerate((0, rows)):
        opened = ext[1, f : f + 1] * ext[1, f + 1 : f + 2]
        ext[10, n : n + 1] = opened
        ext[10, n + 2 : n + 3] = opened * (0.5 * (ext[0, f : f + 1] + ext[0, f + 1 : f + 2]))

    def put_lon(i, block):
        (opx, odx)[i // 2][(0, rows)[i % 2], 0:cells] = block

    spread(turned(ext[10, 0:rows])[0:cells], 4, put_lon)

    def with_ends(own, south, north):
        mine = jnp.where(lane == cells, pltpu.roll(own, cells, axis=1), own)
        other = jnp.where(lane == cells - 1, pltpu.roll(north, cells - 1, axis=1), ahead_of(own))
        return mine, jnp.where(lane == cells, pltpu.roll(south, 1, axis=1), other)

    sea_a, sea_b = with_ends(ext[3, 0:rows], ext[5, 0:rows], ext[7, 0:rows])
    cy_a, cy_b = with_ends(ext[2, 0:rows], ext[4, 0:rows], ext[6, 0:rows])
    closed = jnp.logical_or(
        jnp.logical_and(lane == cells, jnp.logical_not(has_south)),
        jnp.logical_and(lane == cells - 1, jnp.logical_not(has_north)),
    )
    opened = jnp.where(closed, 0.0, sea_a * sea_b)
    drift = jnp.where(closed, 0.0, opened * (0.5 * (cy_a + cy_b)))
    wide = slice(cells - TILE, cells + TILE)

    def put_lat(i, block):
        opy[i, wide] = block[0 : 2 * TILE]
        ody[i, wide] = block[2 * TILE : 4 * TILE]

    spread(jnp.concatenate([turned(opened)[wide], turned(drift)[wide]], axis=0), rows, put_lat)

    settle(adj.at[pl.ds(0, 2)], load_sem.at[6 + len(groups)])

    def edge_piece(p):
        settle(recv_s.at[p], recv_sem.at[2 + p])
        edge(p)

    middle = order[:-2]
    cut = (len(middle) + 1) // 2
    for p in middle[:cut]:
        edge_piece(p)
    for n, (a, b) in enumerate(lat_groups):
        first_arrives(n)
        lax.fori_loop((a - 1) // 2, (b - 1) // 2, outer_pair, 0)
        lat_start(lambda side, n=n: side.second[n])
        if n == 0:
            for p in middle[cut:]:
                edge_piece(p)
    for p in order[-2:]:
        edge_piece(p)
    lat_start(lambda side: side.second[2])

    def back(r, chunk, lo, hi, west_t, east_t):
        c, s, w = chunk
        own = tt[r, c, 8 + lo : 8 + hi, 0:w]
        value = own + jnp.maximum(cxs[r + 1, c, lo:hi, 0:w], 0.0) * (east_t - own)
        value = value + jnp.minimum(cxs[r, c, lo:hi, 0:w], 0.0) * (own - west_t)
        value = value + jnp.maximum(cys[r, c, 8 + lo : 8 + hi, 0:w], 0.0) * (tt[r, c, 9 + lo : 9 + hi, 0:w] - own)
        value = value + jnp.minimum(cys[r, c, 7 + lo : 7 + hi, 0:w], 0.0) * (own - tt[r, c, 7 + lo : 7 + hi, 0:w])
        done[r, lo:hi, s : s + w] = value

    def back_row(segments):
        def one(r, carry):
            for chunk in chunks:
                c, _, w = chunk
                for lo, hi in segments:
                    near = [tt[r + d, c, 8 + lo : 8 + hi, 0:w] for d in (-1, 1)]
                    back(r, chunk, lo, hi, *near)
            return carry

        return one

    lax.fori_loop(1, rows - 1, back_row(inner), 0)
    for n, (a, b) in enumerate(lat_groups):
        second_arrives(n)
        lax.fori_loop(a, b, back_row(outer), 0)
    second_arrives(2)
    for p in order:
        settle(recv_t.at[p], recv_sem.at[2 + tiles + p])
        lo, hi = TILE * p, TILE * p + TILE
        for chunk in chunks:
            c, _, w = chunk
            back(0, chunk, lo, hi, unpack(plan_neg, chunk, recv_t.at[p, 0]), tt[1, c, 8 + lo : 8 + hi, 0:w])
            back(rows - 1, chunk, lo, hi, tt[rows - 2, c, 8 + lo : 8 + hi, 0:w], unpack(plan_pos, chunk, recv_t.at[p, 1]))

    for n, ref in enumerate((face_f, face_i, send_s, send_t)):
        settle(ref, send_sem.at[n])
    for side, edge_rim in zip(lat_all, (rim.at[1], rim.at[0])):
        @pl.when(side.there)
        def _(side=side, edge_rim=edge_rim):
            for copy in side.small:
                copy.wait_send()
            settle(edge_rim, send_sem.at[side.out + 2])
            settle(tt.at[:, :, pl.ds(side.own, 1)], send_sem.at[side.out + 3])


def keep(array):
    return pltpu.with_memory_space_constraint(array, pltpu.HBM)


def round_up(value, step):
    return (value + step - 1) // step * step


def body(nx, ny, spectrum, adjoint_in, cx, cy, wx, wy, land, ice, speed, growth, diss):
    rows, cells, bins = spectrum.shape
    freqs = speed.shape[0]
    angles = 2.0 * math.pi / DIRS * (np.arange(DIRS) + 0.5)
    cosine, sine = (np.repeat(f(angles), freqs) for f in (np.cos, np.sin))
    plan_pos, plan_neg = slot_plan(cosine > -CERTAIN), slot_plan(cosine < CERTAIN)
    slots = max(len(plan_pos), len(plan_neg))
    many = round_up(freqs, 16)
    hot = (np.arange(many)[:, None] == np.arange(bins)[None] % freqs).astype(np.float32)
    consts = np.concatenate([hot, np.tile(cosine, (TILE, 1)), np.tile(sine, (TILE, 1))]).astype(np.float32)
    tiles, width = cells // TILE, -(-bins // LANES)
    tall = round_up(rows + 2, 8)
    first = 1 + 2 * ((rows - 2) // 4 + 1)
    lat_groups = ((1, first), (first, rows - 1))
    f32 = jnp.float32
    dma = pltpu.SemaphoreType.DMA
    vmem = lambda *shape: pltpu.VMEM(shape, f32)
    return pl.pallas_call(
        functools.partial(kernel, nx, ny, plan_pos, plan_neg, lat_groups),
        out_shape=jax.ShapeDtypeStruct((rows, cells, bins), f32),
        in_specs=[HBM] * 12,
        out_specs=VMEM,
        scratch_shapes=[
            vmem(2, rows, cells, bins),
            vmem(2, rows, 1, bins),
            vmem(2, rows, 1, bins),
            vmem(rows, width, cells + 16, LANES),
            vmem(rows + 1, width, cells, LANES),
            vmem(2, width, cells, LANES),
            vmem(rows, width, cells + 8, LANES),
            vmem(5, width, TILE, LANES),
            vmem(rows + 1, cells, LANES),
            vmem(rows + 1, cells, LANES),
            vmem(rows, cells + TILE, LANES),
            vmem(rows, cells + TILE, LANES),
            vmem(rows, cells, LANES),
            vmem(rows, cells, LANES),
            vmem(rows, cells, LANES),
            vmem(tiles, 2, slots, TILE, LANES),
            vmem(tiles, 2, slots, TILE, LANES),
            vmem(tiles, 2, slots, TILE, LANES),
            vmem(tiles, 2, slots, TILE, LANES),
            vmem(4, rows, cells),
            pltpu.VMEM((2, rows, cells), jnp.int32),
            vmem(2, rows, cells),
            pltpu.VMEM((2, rows, cells), jnp.int32),
            vmem(2, TILE, cells),
            pltpu.VMEM((2, TILE, cells), jnp.int32),
            vmem(3, 1, freqs),
            vmem(many + 2 * TILE, bins),
            vmem(3 * TILE, many),
            vmem(11, tall, LANES),
            vmem(8, width, cells + 8, LANES),
            dma((11,)),
            dma((12,)),
            dma((2 + 2 * tiles + 14,)),
        ],
        compiler_params=pltpu.CompilerParams(
            collective_id=0, has_side_effects=True, vmem_limit_bytes=40 * 2**20
        ),
        name="step",
    )(*map(keep, (spectrum, adjoint_in, cx, cy, wx, wy, land, ice)),
      *map(keep, (speed.reshape(1, -1), growth.reshape(1, -1), diss.reshape(1, -1), jnp.asarray(consts))))


def solution(mesh):
    grid = P("gx", "gy")
    field = P("gx", "gy", None)
    return jax.shard_map(
        functools.partial(body, mesh.shape["gx"], mesh.shape["gy"]),
        mesh=mesh,
        in_specs=(field, field) + (grid,) * 6 + (P(), P(), P()),
        out_specs=field,
        check_vma=False,
    )
```

profile of v0, /device:TPU:0, one launch (start us, length us, event | category | flops | bytes accessed | tf_op | source)
XLA Modules:
  0.0 21.0 jit_solution(2986668384655978717)
XLA Ops:
  0.0 18.9 %step.1 = f32[24,40,1080]{2,1,0:T(8,128)S(1)} custom-call(f32[24,40,1080]{2,1,0:T(8,128)} %spectrum.1, f32[24,40,1080]{2,1,0:T(8,128)} %adjoint.1, f32[24,40]{1,0:T(8,128)} %cx_h.1, f32[24,40]{1,0:T(8,128)} %cy_h.1, f32[24,40]{1,0:T(8,128)} %wx_h.1, f32[24,40]{1,0:T(8,128)} %wy_h.1, s32[24,40]{1,0:T(8,128)} %land_h.1, s32[24,40]{1,0:T(8,128)} %ice_h.1, ...), custom_call_target="tpu_custom_call" | custom-call | tf_op jit(solution)/shard_map/step/pallas_call | solution.py:611
  18.9 2.1 %copy.14 = f32[24,40,1080]{2,1,0:T(8,128)} copy(f32[24,40,1080]{2,1,0:T(8,128)S(1)} %step.1) | data formatting | bytes 8294400
where the time goes:
time: 21.1 us; the launch traced here: 21 us
  Pallas kernels  18.9 us (90%)
  local copies, waits for them, and re-layouts  2.09 us (10%)
    pallas_call x1, Pallas kernels, body(): pl.pallas_call(functools.partial(kernel, nx, ny, plan_pos, plan_neg, lat_...  18.9 us
    unnamed x1, local copies, waits for them, and re-layouts  2.09 us

commit v1 on v0

v1 whole, which is shorter than its diff:
```python
import functools
import math
from types import SimpleNamespace

import jax
import jax.numpy as jnp
import numpy as np
from jax import lax
from jax.experimental import pallas as pl
from jax.experimental.pallas import tpu as pltpu
from jax.sharding import PartitionSpec as P

DIRS = 36
LANES = 128
TILE = 8
CERTAIN = 0.81
HBM = pl.BlockSpec(memory_space=pltpu.HBM)
VMEM = pl.BlockSpec(memory_space=pltpu.VMEM)
MESH = pl.DeviceIdType.MESH


def lane_chunks(bins):
    return [(c, s, min(LANES, bins - s)) for c, s in enumerate(range(0, bins, LANES))]


def slot_plan(need):
    parts = []
    for c, s, w in lane_chunks(len(need)):
        lane = 0
        while lane < w:
            if not need[s + lane]:
                lane += 1
                continue
            first = lane
            while lane < w and need[s + lane]:
                lane += 1
            parts.append((c, first, lane, w))
    parts.sort(key=lambda p: (p[3] == LANES, p[1] - p[2]))
    slots, used = [], []
    for c, first, last, w in parts:
        size = last - first
        for n, busy in enumerate(used):
            if not busy[first:last].any():
                shift = 0
            elif w == LANES:
                starts = [k for k in range(LANES - size + 1) if not busy[k : k + size].any()]
                if not starts:
                    continue
                shift = starts[0] - first
            else:
                continue
            busy[first + shift : last + shift] = True
            slots[n].append((c, first, last, shift % LANES))
            break
        else:
            busy = np.zeros(LANES, bool)
            busy[first:last] = True
            used.append(busy)
            slots.append([(c, first, last, 0)])
    return slots


def repeat(value, count):
    return value if count == 1 else jnp.concatenate([value] * count, axis=0)


def between(first, last):
    lane = lax.broadcasted_iota(jnp.int32, (TILE, LANES), 1)
    return jnp.logical_and(lane >= first, lane < last)


def pack(plan, chunks, load, out):
    for n, parts in enumerate(plan):
        value, late = None, None
        for c, first, last, shift in parts:
            w = chunks[c][2]
            if w < LANES:
                late = (c, w)
                continue
            part = load(c)
            if shift:
                part = pltpu.roll(part, shift, axis=1)
            begin = (first + shift) % LANES
            value = part if value is None else jnp.where(between(begin, begin + last - first), part, value)
        if value is not None:
            out[n] = value
        if late is not None:
            out[n, :, 0 : late[1]] = load(late[0])


def unpack(plan, chunk, slots):
    c, _, w = chunk
    value = jnp.zeros((TILE, w), jnp.float32)
    for n, parts in enumerate(plan):
        for chunk_of, first, last, shift in parts:
            if chunk_of != c:
                continue
            if w < LANES:
                part = slots[n, :, 0:w]
                if last - first < w:
                    part = jnp.where(between(first, last)[:, 0:w], part, 0.0)
                value = part
                continue
            part = slots[n]
            if shift:
                part = pltpu.roll(part, LANES - shift, axis=1)
            value = part if last - first == LANES else jnp.where(between(first, last), part, value)
    return value


def split3(value):
    high = value.astype(jnp.bfloat16).astype(jnp.float32)
    rest = value - high
    mid = rest.astype(jnp.bfloat16).astype(jnp.float32)
    return [high, mid, rest - mid]


def kernel(
    nx, ny, plan_pos, plan_neg,
    spectrum, adjoint, cx_h, cy_h, wx_h, wy_h, land_h, ice_h, speed_h, growth_h, diss_h, consts_h,
    done,
    both, rim, own_c, halo_c, adj_c, part_c, face_c, mine_c, next_c, cst, tt, cxs, fxs, cys, tab, opx, odx, opy, ody, wxs, wys, seas,
    send_s, recv_s, send_t, recv_t, mine_f, mine_i, near_f, near_i, face_f, face_i, coeffs, consts, params, ext, bufs, load_sem, send_sem, recv_sem,
):
    gx, gy = lax.axis_index("gx"), lax.axis_index("gy")
    rows, cells, bins = adjoint.shape
    east, west = lax.rem(gx + 1, nx), lax.rem(gx + nx - 1, nx)
    has_north, has_south = gy < ny - 1, gy > 0
    chunks = lane_chunks(bins)
    tiles = cells // TILE
    f32 = jnp.float32
    sp, adj = both.at[0], both.at[1]

    cx, cy, wx, wy = (mine_f.at[m] for m in range(4))
    land, ice = (mine_i.at[m] for m in range(2))
    speed, growth, diss = (coeffs.at[m] for m in range(3))
    pairs = (rows - 2) // 2
    bounds = [1, 4, 10, 16, rows - 1]
    local = lambda src, dst, n: pltpu.make_async_copy(src, dst, load_sem.at[n])
    ends = [local(spectrum.at[r], sp.at[r], 0) for r in (0, rows - 1)]
    small = [
        local(src, dst, n)
        for src, dst, n in (
            (cx_h, cx, 1), (cy_h, cy, 1), (wx_h, wx, 1), (wy_h, wy, 1), (land_h, land, 2), (ice_h, ice, 2),
            (speed_h, speed, 3), (growth_h, growth, 3), (diss_h, diss, 3), (consts_h, consts, 4),
        )
    ]
    rims = [
        local(spectrum.at[:, pl.ds(0, 1), :], rim.at[0], 5),
        local(spectrum.at[:, pl.ds(cells - 1, 1), :], rim.at[1], 5),
    ]
    groups = []
    for n, (a, b) in enumerate(zip(bounds[:-1], bounds[1:])):
        groups.append(
            [local(src.at[pl.ds(a, b - a)], dst.at[pl.ds(a, b - a)], 6 + n) for src, dst in ((spectrum, sp), (adjoint, adj))]
        )
    last_adj = [local(adjoint.at[r], adj.at[r], 6 + len(groups)) for r in (0, rows - 1)]
    for copy in ends + small + rims:
        copy.start()

    barrier = pltpu.get_barrier_semaphore()
    for where in (east, west):
        pl.semaphore_signal(barrier, inc=1, device_id={"gx": where}, device_id_type=MESH)

    @pl.when(has_north)
    def _():
        pl.semaphore_signal(barrier, inc=1, device_id={"gy": gy + 1}, device_id_type=MESH)

    @pl.when(has_south)
    def _():
        pl.semaphore_signal(barrier, inc=1, device_id={"gy": gy - 1}, device_id_type=MESH)

    for group in groups:
        for copy in group:
            copy.start()
    for copy in last_adj:
        copy.start()

    def far(src, dst, out, n, axis, where):
        return pltpu.make_async_remote_copy(
            src_ref=src, dst_ref=dst, send_sem=send_sem.at[out], recv_sem=recv_sem.at[n],
            device_id={axis: where}, device_id_type=MESH,
        )

    def settle(ref, sem):
        pltpu.make_async_copy(ref, ref, sem).wait()

    order = list(range(1, tiles - 1)) + [0, tiles - 1]
    ahead = []
    for m, (src, dst) in enumerate(((cx, face_f), (land, face_i))):
        ahead.append(far(src.at[pl.ds(rows - TILE, TILE)], dst.at[0], m, m, "gx", east))
        ahead.append(far(src.at[pl.ds(0, TILE)], dst.at[1], m, m, "gx", west))
    lon_s, lon_t = (
        [[far(src.at[p, d], dst.at[p, d], 2 + m, 2 + m * tiles + p, "gx", (east, west)[d]) for d in range(2)] for p in range(tiles)]
        for m, (src, dst) in enumerate(((send_s, recv_s), (send_t, recv_t)))
    )
    tops = rows // TILE
    span = lambda g: pl.ds(TILE * g, TILE)
    lat_all = []
    for d, (where, there, back_there) in enumerate(((gy + 1, has_north, has_south), (gy - 1, has_south, has_north))):
        sem = 2 + 2 * tiles + (2 + 2 * tops) * d
        away = lambda src, dst, out, n, where=where, d=d, sem=sem: far(src, dst, 4 + 4 * d + out, sem + n, "gy", where)
        lat_all.append(SimpleNamespace(
            there=there, back_there=back_there, out=4 + 4 * d,
            small=[away(cy, near_f.at[d], 0, 0), away(land, near_i.at[d], 1, 1)],
            first=[away(own_c.at[1 - d, :, span(g)], halo_c.at[d, :, span(g)], 2, 2 + g) for g in range(tops)],
            second=[away(mine_c.at[1 - d, :, span(g)], next_c.at[d, :, span(g)], 3, 2 + tops + g) for g in range(tops)],
        ))

    def lat_start(pick):
        for side in lat_all:
            @pl.when(side.there)
            def _(side=side):
                for copy in pick(side):
                    copy.start()

    def lat_arrive(pick):
        for side in lat_all:
            @pl.when(side.back_there)
            def _(side=side):
                pick(side)

    def first_arrives(n):
        lat_arrive(lambda side: side.first[n].wait_recv())

    def second_arrives(n):
        lat_arrive(lambda side: side.second[n].wait_recv())

    settle(sp.at[pl.ds(0, 2)], load_sem.at[0])
    for p in range(tiles):
        for d, (row, plan) in enumerate(((rows - 1, plan_pos), (0, plan_neg))):
            load = lambda c, row=row, p=p: sp[row, TILE * p : TILE * p + TILE, chunks[c][1] : chunks[c][1] + chunks[c][2]]
            pack(plan, chunks, load, send_s.at[p, d])
    for n, ref in enumerate((mine_f, mine_i, coeffs, consts, rim)):
        settle(ref, load_sem.at[1 + n])

    nil = jnp.zeros((1, LANES), f32)

    def prepare(r, carry):
        for c, s, w in chunks:
            for d in range(2):
                own_c[d, c, pl.ds(r, 1), 0:w] = rim[d, r, :, s : s + w]
            tt[r, c, 7:8] = nil
            tt[r, c, 8 + cells : 9 + cells] = nil
            cys[r, c, 7:8] = nil
        return carry

    lax.fori_loop(0, rows, prepare, 0)
    for q in range(2):
        for c, _, _ in chunks:
            bufs[4 * q, c, cells : cells + 1] = nil
            bufs[4 * q + 1, c, 7:8] = nil
    freqs = coeffs.shape[2]
    params[...] = jnp.zeros(params.shape, f32)
    for m, ref in enumerate((speed, growth, diss)):
        params[TILE * m : TILE * m + TILE, 0:freqs] = jnp.broadcast_to(ref[...], (TILE, freqs))
    many = params.shape[1]
    hot = consts[0:many].astype(jnp.bfloat16)
    by_bin = sum(
        jnp.dot(part.astype(jnp.bfloat16), hot, preferred_element_type=f32) for part in split3(params[...])
    )
    cosine, sine = consts[many : many + TILE], consts[many + TILE : many + 2 * TILE]
    for c, s, w in chunks:
        cs = slice(s, s + w)
        tab[0, c, :, 0:w] = by_bin[0:TILE, cs] * cosine[:, cs]
        tab[1, c, :, 0:w] = by_bin[0:TILE, cs] * sine[:, cs]
        tab[2, c, :, 0:w] = by_bin[TILE : 2 * TILE, cs] * cosine[:, cs]
        tab[3, c, :, 0:w] = by_bin[TILE : 2 * TILE, cs] * sine[:, cs]
        tab[4, c, :, 0:w] = by_bin[2 * TILE : 3 * TILE, cs]

    sub = lax.broadcasted_iota(jnp.int32, (LANES, 2 * LANES), 0)
    half = (lax.broadcasted_iota(jnp.int32, (LANES, 2 * LANES), 1) >= LANES).astype(jnp.int32)
    row_of = jnp.where(sub < rows, sub, jnp.where(sub < 2 * rows, sub - rows, jnp.where(sub < 3 * rows, sub - 2 * rows, -2)))
    row_of = row_of - half

    def turned(field):
        stack = split3(field)
        stack.append(jnp.zeros((LANES - 3 * rows, LANES), f32))
        return jnp.concatenate(stack, axis=0).T

    def spread(lhs, count, put):
        lhs = lhs.astype(jnp.bfloat16)
        for n in range(count // 2):
            pick = jnp.where(row_of == 2 * n, 1.0, 0.0).astype(jnp.bfloat16)
            out = jnp.dot(lhs, pick, preferred_element_type=f32)
            put(2 * n, out[:, 0:LANES])
            put(2 * n + 1, out[:, LANES:])

    sea_of = lambda mask: (1 - mask).astype(f32)
    ext[...] = jnp.zeros(ext.shape, f32)
    ice_free = sea_of(ice[...])
    ext[0, 1 : rows + 1, 0:cells] = cx[...]
    ext[1, 1 : rows + 1, 0:cells] = sea_of(land[...])
    ext[2, 0:rows, 0:cells] = cy[...]
    ext[3, 0:rows, 0:cells] = sea_of(land[...])
    windy = ice_free * sea_of(land[...])
    ext[8, 0:rows, 0:cells] = wx[...] * windy
    ext[9, 0:rows, 0:cells] = wy[...] * windy
    lane = lax.broadcasted_iota(jnp.int32, (rows, LANES), 1)
    sea, drift = ext[3, 0:rows], ext[2, 0:rows]
    opened_x = ext[1, 0:rows] * ext[1, 1 : rows + 1]
    ahead_of = lambda value: pltpu.roll(value, LANES - 1, axis=1)
    opened_y = sea * ahead_of(sea)
    fields = [
        opened_x, opened_x * (0.5 * (ext[0, 0:rows] + ext[0, 1 : rows + 1])),
        opened_y, opened_y * (0.5 * (drift + ahead_of(drift))),
        ext[8, 0:rows], ext[9, 0:rows], sea,
    ]
    homes = (opx, odx, opy, ody, wxs, wys, seas)

    def put_all(i, block):
        for k, home in enumerate(homes):
            home[i, 0:cells] = block[k * cells : (k + 1) * cells]

    spread(jnp.concatenate([turned(f)[0:cells] for f in fields], axis=0), rows, put_all)

    for m, field in enumerate((ext[8, 0:rows], ext[9, 0:rows], sea)):
        for d, cell in enumerate((0, cells - 1)):
            cst[d, 2 + m] = jnp.broadcast_to(field[:, cell : cell + 1], (rows, LANES))
    for d, there in enumerate((has_south, has_north)):
        @pl.when(jnp.logical_not(there))
        def _(d=d):
            halo_c[d] = jnp.zeros(halo_c.shape[1:], f32)
            next_c[d] = jnp.zeros(next_c.shape[1:], f32)

    def lat_part(buf, r, chunk, lo, own, fields, first, last, ends):
        c, s, w = chunk
        hi = lo + TILE
        sine_row = tab[1, c, :, 0:w]
        if first:
            buf.near[c, lo:hi, 0:w] = own
        if not last:
            buf.near[c, hi : hi + TILE, 0:w] = sp[r, hi : hi + TILE, s : s + w]
        elif hi < cells:
            buf.near[c, hi : hi + 1, 0:w] = sp[r, hi : hi + 1, s : s + w]
        elif ends:
            buf.near[c, hi : hi + 1, 0:w] = halo_c[1, c, r : r + 1, 0:w]
        upper = buf.near[c, lo + 1 : hi + 1, 0:w]
        courant = fields[0][:, 0:w] * sine_row + fields[1][:, 0:w]
        cys[r, c, 8 + lo : 8 + hi, 0:w] = courant
        fy = courant * jnp.where(courant > 0, own, upper)
        buf.flux[c, 8 + lo : 8 + hi, 0:w] = fy
        if first and (lo or ends):
            if lo:
                low = opy[r, lo - 1 : lo, 0:w] * sine_row[0:1] + ody[r, lo - 1 : lo, 0:w]
                below = sp[r, lo - 1 : lo, s : s + w]
            else:
                low = cst[0, 0, r : r + 1, 0:w] * sine_row[0:1] + cst[0, 1, r : r + 1, 0:w]
                below = halo_c[0, c, r : r + 1, 0:w]
                cys[r, c, 7 + lo : 8 + lo, 0:w] = low
            buf.flux[c, 7 + lo : 8 + lo, 0:w] = low * jnp.where(low > 0, below, own[0:1])
        return fy - buf.flux[c, 7 + lo : 7 + hi, 0:w]

    def lon_cells(f, lo):
        return opx[f, lo : lo + TILE], odx[f, lo : lo + TILE]

    def lon_speed(f, chunk, lo, fields):
        c, _, w = chunk
        speed = fields[0][:, 0:w] * tab[0, c, :, 0:w] + fields[1][:, 0:w]
        cxs[f, c, lo : lo + TILE, 0:w] = speed
        return speed

    def upwind(speed, here, there):
        return speed * jnp.where(speed > 0, here, there)

    def gather(totals, rest):
        value = jnp.sum(totals, axis=1, keepdims=True)
        return value if rest is None else value + rest

    def mean(sums):
        return jnp.broadcast_to(gather(*sums) * (1.0 / bins), (TILE, LANES))

    def weigh(chunk, advected, incoming, energy, wind_x, wind_y, open_sea, sums):
        c, _, w = chunk
        blow = wind_x[:, 0:w] * tab[2, c, :, 0:w] + wind_y[:, 0:w] * tab[3, c, :, 0:w]
        gain = open_sea[:, 0:w] + jnp.maximum(blow, 0.0)
        scaled = tab[4, c, :, 0:w] * advected
        damp = 1.0 + energy[:, 0:w] * scaled
        weighted = incoming * gain / (damp * damp)
        return weighted, add_up(chunk, weighted * scaled * advected, *sums)

    def add_up(chunk, value, total, rest):
        if chunk[2] == LANES:
            return total + value, rest
        return total, jnp.sum(value, axis=1, keepdims=True)

    none = (jnp.zeros((TILE, LANES), f32), None)
    slots = [SimpleNamespace(near=bufs.at[4 * q], flux=bufs.at[4 * q + 1], moved=bufs.at[4 * q + 2], weight=bufs.at[4 * q + 3]) for q in range(4)]

    def source(bufs_of, rows_of, lo, sums):
        hi = lo + TILE
        energy = [mean(each) for each in sums]
        sums = [none for _ in sums]
        fields = [(wxs[r, lo:hi], wys[r, lo:hi], seas[r, lo:hi]) for r in rows_of]
        for chunk in chunks:
            c, s, w = chunk
            for q, (buf, r) in enumerate(zip(bufs_of, rows_of)):
                weighted, sums[q] = weigh(chunk, buf.moved[c, lo:hi, 0:w], adj[r, lo:hi, s : s + w], energy[q], *fields[q], sums[q])
                buf.weight[c, lo:hi, 0:w] = weighted
        yield
        coupling = [mean(each) for each in sums]
        for c, s, w in chunks:
            for q, (buf, r) in enumerate(zip(bufs_of, rows_of)):
                tt[r, c, 8 + lo : 8 + hi, 0:w] = buf.weight[c, lo:hi, 0:w] - coupling[q][:, 0:w]
        yield

    def stagger(first, jobs):
        running = []
        for step in range(len(jobs) + 2):
            if step < len(jobs):
                running.append(first(jobs[step]))
            for n in (step - 1, step - 2):
                if 0 <= n < len(jobs):
                    next(running[n])

    def row_pair(r, chosen):
        def advance(a):
            lo, hi = TILE * a, TILE * a + TILE
            first, last = a - 1 not in chosen, a + 1 not in chosen
            sums = [none, none]
            lon = [lon_cells(r + q + 1, lo) for q in range(2)]
            lat = [(opy[r + q, lo:hi], ody[r + q, lo:hi]) for q in range(2)]
            for chunk in chunks:
                c, s, w = chunk
                own = [sp[r + q, lo:hi, s : s + w] for q in range(3)]
                flux_west = fxs[0, c, lo:hi, 0:w]
                for q in range(2):
                    buf = slots[q]
                    flux = upwind(lon_speed(r + q + 1, chunk, lo, lon[q]), own[q], own[q + 1])
                    if q:
                        fxs[0, c, lo:hi, 0:w] = flux
                    moved = own[q] - (flux - flux_west) - lat_part(buf, r + q, chunk, lo, own[q], lat[q], first, last, False)
                    flux_west = flux
                    for d, cell in enumerate((0, cells - 1)):
                        if cell // TILE == a:
                            part_c[d, c, pl.ds(r + q, 1), 0:w] = moved[cell - lo : cell - lo + 1]
                            adj_c[d, c, pl.ds(r + q, 1), 0:w] = adj[r + q, cell : cell + 1, s : s + w]
                    buf.moved[c, lo:hi, 0:w] = moved
                    sums[q] = add_up(chunk, moved, *sums[q])
            return source(slots[0:2], (r, r + 1), lo, sums)

        stagger(advance, chosen)

    def edge(pieces):
        def advance(p):
            lo, hi = TILE * p, TILE * p + TILE
            sums = [none, none]
            lon = [lon_cells(f, lo) for f in (0, rows - 1, rows)]
            lat = [(opy[r, lo:hi], ody[r, lo:hi]) for r in (0, rows - 1)]
            for chunk in chunks:
                c, s, w = chunk
                for q, r in enumerate((0, rows - 1)):
                    own = sp[r, lo:hi, s : s + w]
                    if q == 0:
                        flux_west = upwind(lon_speed(0, chunk, lo, lon[0]), unpack(plan_pos, chunk, recv_s.at[p, 0]), own)
                        flux = fxs[1, c, lo:hi, 0:w]
                    else:
                        before = lon_speed(rows - 1, chunk, lo, lon[1])
                        flux_west = upwind(before, sp[rows - 2, lo:hi, s : s + w], own)
                        flux = upwind(lon_speed(rows, chunk, lo, lon[2]), own, unpack(plan_neg, chunk, recv_s.at[p, 1]))
                    moved = own - (flux - flux_west) - lat_part(slots[2 + q], r, chunk, lo, own, lat[q], p == 0, p == tiles - 1, True)
                    slots[2 + q].moved[c, lo:hi, 0:w] = moved
                    sums[q] = add_up(chunk, moved, *sums[q])
            return source(slots[2:4], (0, rows - 1), lo, sums)

        for p in pieces:
            settle(recv_s.at[p], recv_sem.at[2 + p])
        stagger(advance, pieces)
        for p in pieces:
            lo, hi = TILE * p, TILE * p + TILE
            for d, (row, plan) in enumerate(((rows - 1, plan_neg), (0, plan_pos))):
                pack(plan, chunks, lambda c, row=row: tt[row, c, 8 + lo : 8 + hi, 0 : chunks[c][2]], send_t.at[p, d])
            for copy in lon_t[p]:
                copy.start()

    def ends_of(groups_of):
        jobs = [(g, d) for g in groups_of for d in range(2)]

        def advance(job):
            g, d = job
            at, sums = slice(TILE * g, TILE * g + TILE), none
            for chunk in chunks:
                c, _, w = chunk
                courant = cst[d, 0, at, 0:w] * tab[1, c, :, 0:w] + cst[d, 1, at, 0:w]
                face_c[d, c, at, 0:w] = courant
                own, halo = own_c[d, c, at, 0:w], halo_c[d, c, at, 0:w]
                flux = upwind(courant, halo, own) if d == 0 else -upwind(courant, own, halo)
                moved = part_c[d, c, at, 0:w] + flux
                part_c[d, c, at, 0:w] = moved
                sums = add_up(chunk, moved, *sums)
            return finish(g, d, sums)

        def finish(g, d, sums):
            at = slice(TILE * g, TILE * g + TILE)
            energy, sums = mean(sums), none
            for chunk in chunks:
                c, _, w = chunk
                mine_c[d, c, at, 0:w], sums = weigh(
                    chunk, part_c[d, c, at, 0:w], adj_c[d, c, at, 0:w], energy, cst[d, 2, at], cst[d, 3, at], cst[d, 4, at], sums
                )
            yield
            coupling = mean(sums)
            for c, _, w in chunks:
                mine_c[d, c, at, 0:w] = mine_c[d, c, at, 0:w] - coupling[:, 0:w]
            yield

        stagger(advance, jobs)
        for g in groups_of:
            for r in range(TILE * g, TILE * g + TILE):
                for c, _, w in chunks:
                    for d, cell in enumerate((0, cells - 1)):
                        if 0 < r < rows - 1:
                            tt[r, c, 8 + cell : 9 + cell, 0:w] = mine_c[d, c, r : r + 1, 0:w]

    def send_ends(g):
        for r in (0, rows - 1):
            if r // TILE == g:
                for c, _, w in chunks:
                    for d, cell in enumerate((0, cells - 1)):
                        mine_c[d, c, r : r + 1, 0:w] = tt[r, c, 8 + cell : 9 + cell, 0:w]
        lat_start(lambda side: [side.second[g]])

    def wait_group(n):
        settle(both.at[:, pl.ds(bounds[n], bounds[n + 1] - bounds[n])], load_sem.at[6 + n])

    wait_group(0)
    for lo in range(0, cells, TILE):
        lon = lon_cells(1, lo)
        for chunk in chunks:
            c, s, w = chunk
            flux = upwind(lon_speed(1, chunk, lo, lon), sp[0, lo : lo + TILE, s : s + w], sp[1, lo : lo + TILE, s : s + w])
            for m in range(2):
                fxs[m, c, lo : lo + TILE, 0:w] = flux

    pl.semaphore_wait(barrier, 2 + has_north.astype(jnp.int32) + has_south.astype(jnp.int32))
    for copy in ahead:
        copy.start()
    lat_start(lambda side: side.small)
    for p in order:
        for copy in lon_s[p]:
            copy.start()
    lat_start(lambda side: side.first)

    firsts = [next(k for k in range(pairs + 1) if 3 + 2 * k >= b) for b in bounds[1:-1]]

    def halo_faces():
        for m, ref in enumerate((face_f, face_i)):
            settle(ref, recv_sem.at[m])
        lat_arrive(lambda side: [copy.wait_recv() for copy in side.small])
        ext[0, 0:1, 0:cells] = face_f[0, TILE - 1 : TILE]
        ext[0, rows + 1 : rows + 2, 0:cells] = face_f[1, 0:1]
        ext[1, 0:1, 0:cells] = sea_of(face_i[0, TILE - 1 : TILE])
        ext[1, rows + 1 : rows + 2, 0:cells] = sea_of(face_i[1, 0:1])
        ext[4, 0:rows, 0:cells] = near_f[0]
        ext[5, 0:rows, 0:cells] = sea_of(near_i[0])
        ext[6, 0:rows, 0:cells] = near_f[1]
        ext[7, 0:rows, 0:cells] = sea_of(near_i[1])
        for n, f in enumerate((0, rows)):
            opened = ext[1, f : f + 1] * ext[1, f + 1 : f + 2]
            ext[10, n : n + 1] = opened
            ext[10, n + 2 : n + 3] = opened * (0.5 * (ext[0, f : f + 1] + ext[0, f + 1 : f + 2]))

        def put_lon(i, block):
            (opx, odx)[i // 2][(0, rows)[i % 2], 0:cells] = block

        spread(turned(ext[10, 0:rows])[0:cells], 4, put_lon)

        def with_ends(own, south, north):
            mine = jnp.where(lane == cells, pltpu.roll(own, cells, axis=1), own)
            other = jnp.where(lane == cells - 1, pltpu.roll(north, cells - 1, axis=1), ahead_of(own))
            return mine, jnp.where(lane == cells, pltpu.roll(south, 1, axis=1), other)

        sea_a, sea_b = with_ends(ext[3, 0:rows], ext[5, 0:rows], ext[7, 0:rows])
        cy_a, cy_b = with_ends(ext[2, 0:rows], ext[4, 0:rows], ext[6, 0:rows])
        closed = jnp.logical_or(
            jnp.logical_and(lane == cells, jnp.logical_not(has_south)),
            jnp.logical_and(lane == cells - 1, jnp.logical_not(has_north)),
        )
        opened = jnp.where(closed, 0.0, sea_a * sea_b)
        drift = jnp.where(closed, 0.0, opened * (0.5 * (cy_a + cy_b)))
        for m, (field, home) in enumerate(((opened, opy), (drift, ody))):
            for d, face in enumerate((cells, cells - 1)):
                cst[d, m] = jnp.broadcast_to(field[:, face : face + 1], (rows, LANES))
            for r in (0, rows - 1):
                home[r, cells - 1 : cells] = cst[1, m, r : r + 1]
        settle(adj.at[pl.ds(0, 2)], load_sem.at[6 + len(groups)])
        for r in (0, rows - 1):
            for c, s, w in chunks:
                for d in range(2):
                    part_c[d, c, r : r + 1, 0:w] = nil[:, 0:w]
                    adj_c[d, c, r : r + 1, 0:w] = nil[:, 0:w]

    cut = pairs // 2 + 1
    every, outer, inner = list(range(tiles)), [0, tiles - 1], list(range(1, tiles - 1))

    def step(chosen):
        def one(k, carry):
            for n, first in enumerate(firsts):
                if chosen != inner:
                    @pl.when(k == first)
                    def _(n=n):
                        wait_group(n + 1)

            row_pair(1 + 2 * k, chosen)
            return carry

        return one

    lax.fori_loop(0, cut, step(every), 0)
    lax.fori_loop(cut, pairs, step(outer), 0)
    for n in range(len(firsts)):
        if firsts[n] >= pairs:
            wait_group(n + 1)
    halo_faces()
    for g in range(tops):
        first_arrives(g)
    edge(every)
    ends_of(range(tops))
    for g in range(tops):
        send_ends(g)
    lax.fori_loop(cut, pairs, step(inner), 0)

    def back(r, count, chunk, lo, west_t, east_t):
        c, s, w = chunk
        hi = lo + TILE
        own = [tt[r + q, c, 8 + lo : 8 + hi, 0:w] for q in range(count)]
        line = [west_t] + own + [east_t]
        steps = [line[q + 1] - line[q] for q in range(count + 1)]
        speeds = [cxs[r + q, c, lo:hi, 0:w] for q in range(count + 1)]
        for q in range(count):
            value = own[q] + jnp.maximum(speeds[q + 1], 0.0) * steps[q + 1]
            value = value + jnp.minimum(speeds[q], 0.0) * steps[q]
            value = value + jnp.maximum(cys[r + q, c, 8 + lo : 8 + hi, 0:w], 0.0) * (tt[r + q, c, 9 + lo : 9 + hi, 0:w] - own[q])
            value = value + jnp.minimum(cys[r + q, c, 7 + lo : 7 + hi, 0:w], 0.0) * (own[q] - tt[r + q, c, 7 + lo : 7 + hi, 0:w])
            done[r + q, lo:hi, s : s + w] = value

    def back_pair(k, carry):
        r = 1 + 2 * k
        for chunk in chunks:
            c, _, w = chunk
            for lo in range(0, cells, TILE):
                near = [tt[r + d, c, 8 + lo : 8 + lo + TILE, 0:w] for d in (-1, 2)]
                back(r, 2, chunk, lo, *near)
        return carry

    lax.fori_loop(0, pairs, back_pair, 0)
    for g in range(tops):
        second_arrives(g)
        rows_of = slice(TILE * g, TILE * g + TILE)
        for d in range(2):
            for c, _, w in chunks:
                courant = face_c[d, c, rows_of, 0:w]
                step = next_c[d, c, rows_of, 0:w] - mine_c[d, c, rows_of, 0:w]
                if d == 0:
                    part_c[d, c, rows_of, 0:w] = -jnp.minimum(courant, 0.0) * step
                else:
                    part_c[d, c, rows_of, 0:w] = jnp.maximum(courant, 0.0) * step
        for r in range(TILE * g, TILE * g + TILE):
            for c, s, w in chunks:
                for d, cell in enumerate((0, cells - 1)):
                    if 0 < r < rows - 1:
                        done[r, cell : cell + 1, s : s + w] = done[r, cell : cell + 1, s : s + w] + part_c[d, c, r : r + 1, 0:w]
                    else:
                        beyond = (7, 8 + cells)[d]
                        tt[r, c, beyond : beyond + 1, 0:w] = next_c[d, c, r : r + 1, 0:w]
    for p in order:
        settle(recv_t.at[p], recv_sem.at[2 + tiles + p])
        lo, hi = TILE * p, TILE * p + TILE
        for chunk in chunks:
            c, _, w = chunk
            back(0, 1, chunk, lo, unpack(plan_neg, chunk, recv_t.at[p, 0]), tt[1, c, 8 + lo : 8 + hi, 0:w])
            back(rows - 1, 1, chunk, lo, tt[rows - 2, c, 8 + lo : 8 + hi, 0:w], unpack(plan_pos, chunk, recv_t.at[p, 1]))

    for n, ref in enumerate((face_f, face_i, send_s, send_t)):
        settle(ref, send_sem.at[n])
    for d, side in enumerate(lat_all):
        @pl.when(side.there)
        def _(d=d, side=side):
            for copy in side.small:
                copy.wait_send()
            settle(own_c.at[1 - d], send_sem.at[side.out + 2])
            settle(mine_c.at[1 - d], send_sem.at[side.out + 3])


def keep(array):
    return pltpu.with_memory_space_constraint(array, pltpu.HBM)


def round_up(value, step):
    return (value + step - 1) // step * step


def body(nx, ny, spectrum, adjoint_in, cx, cy, wx, wy, land, ice, speed, growth, diss):
    rows, cells, bins = spectrum.shape
    freqs = speed.shape[0]
    angles = 2.0 * math.pi / DIRS * (np.arange(DIRS) + 0.5)
    cosine, sine = (np.repeat(f(angles), freqs) for f in (np.cos, np.sin))
    plan_pos, plan_neg = slot_plan(cosine > -CERTAIN), slot_plan(cosine < CERTAIN)
    slots = max(len(plan_pos), len(plan_neg))
    many = round_up(freqs, 16)
    hot = (np.arange(many)[:, None] == np.arange(bins)[None] % freqs).astype(np.float32)
    consts = np.concatenate([hot, np.tile(cosine, (TILE, 1)), np.tile(sine, (TILE, 1))]).astype(np.float32)
    tiles, width = cells // TILE, -(-bins // LANES)
    tall = round_up(rows + 2, 8)
    compact = pltpu.VMEM((2, width, rows, LANES), jnp.float32)
    f32 = jnp.float32
    dma = pltpu.SemaphoreType.DMA
    vmem = lambda *shape: pltpu.VMEM(shape, f32)
    return pl.pallas_call(
        functools.partial(kernel, nx, ny, plan_pos, plan_neg),
        out_shape=jax.ShapeDtypeStruct((rows, cells, bins), f32),
        in_specs=[HBM] * 12,
        out_specs=VMEM,
        scratch_shapes=[
            vmem(2, rows, cells, bins),
            vmem(2, rows, 1, bins),
            compact, compact, compact, compact, compact, compact, compact,
            vmem(2, 5, rows, LANES),
            vmem(rows, width, cells + 16, LANES),
            vmem(rows + 1, width, cells, LANES),
            vmem(2, width, cells, LANES),
            vmem(rows, width, cells + 8, LANES),
            vmem(5, width, TILE, LANES),
            vmem(rows + 1, cells, LANES),
            vmem(rows + 1, cells, LANES),
            vmem(rows, cells, LANES),
            vmem(rows, cells, LANES),
            vmem(rows, cells, LANES),
            vmem(rows, cells, LANES),
            vmem(rows, cells, LANES),
            vmem(tiles, 2, slots, TILE, LANES),
            vmem(tiles, 2, slots, TILE, LANES),
            vmem(tiles, 2, slots, TILE, LANES),
            vmem(tiles, 2, slots, TILE, LANES),
            vmem(4, rows, cells),
            pltpu.VMEM((2, rows, cells), jnp.int32),
            vmem(2, rows, cells),
            pltpu.VMEM((2, rows, cells), jnp.int32),
            vmem(2, TILE, cells),
            pltpu.VMEM((2, TILE, cells), jnp.int32),
            vmem(3, 1, freqs),
            vmem(many + 2 * TILE, bins),
            vmem(3 * TILE, many),
            vmem(11, tall, LANES),
            vmem(16, width, cells + 8, LANES),
            dma((11,)),
            dma((12,)),
            dma((2 + 2 * tiles + 4 + 4 * (rows // TILE),)),
        ],
        compiler_params=pltpu.CompilerParams(
            collective_id=0, has_side_effects=True, vmem_limit_bytes=40 * 2**20
        ),
        name="step",
    )(*map(keep, (spectrum, adjoint_in, cx, cy, wx, wy, land, ice)),
      *map(keep, (speed.reshape(1, -1), growth.reshape(1, -1), diss.reshape(1, -1), jnp.asarray(consts))))


def solution(mesh):
    grid = P("gx", "gy")
    field = P("gx", "gy", None)
    return jax.shard_map(
        functools.partial(body, mesh.shape["gx"], mesh.shape["gy"]),
        mesh=mesh,
        in_specs=(field, field) + (grid,) * 6 + (P(), P(), P()),
        out_specs=field,
        check_vma=False,
    )
```

time: 21.1 us -> 18.8 us (0.89)
  Pallas kernels: 18.9 us -> 16.6 us
    pallas_call x1, Pallas kernels: 18.9 us -> 16.6 us  [body(): pl.pallas_call(functools.partial(kernel, nx, ny, plan_pos, plan_neg), out...]
where the time goes in v1:
time: 18.8 us; the launch traced here: 18.7 us
  Pallas kernels  16.6 us (88%)
  local copies, waits for them, and re-layouts  2.09 us (11%)
    pallas_call x1, Pallas kernels, body(): pl.pallas_call(functools.partial(kernel, nx, ny, plan_pos, plan_neg), out...  16.6 us
    unnamed x1, local copies, waits for them, and re-layouts  2.09 us

profile of v1, /device:TPU:0, one launch (start us, length us, event | category | flops | bytes accessed | tf_op | source)
XLA Modules:
  0.0 18.7 jit_solution(11545432745674200133)
XLA Ops:
  0.0 16.6 %step.1 = f32[24,40,1080]{2,1,0:T(8,128)S(1)} custom-call(f32[24,40,1080]{2,1,0:T(8,128)} %spectrum.1, f32[24,40,1080]{2,1,0:T(8,128)} %adjoint.1, f32[24,40]{1,0:T(8,128)} %cx_h.1, f32[24,40]{1,0:T(8,128)} %cy_h.1, f32[24,40]{1,0:T(8,128)} %wx_h.1, f32[24,40]{1,0:T(8,128)} %wy_h.1, s32[24,40]{1,0:T(8,128)} %land_h.1, s32[24,40]{1,0:T(8,128)} %ice_h.1, ...), custom_call_target="tpu_custom_call" | custom-call | tf_op jit(solution)/shard_map/step/pallas_call | solution.py:709
  16.6 2.1 %copy.14 = f32[24,40,1080]{2,1,0:T(8,128)} copy(f32[24,40,1080]{2,1,0:T(8,128)S(1)} %step.1) | data formatting | bytes 8294400

commit v2 on v1

--- a/solution.py
+++ b/solution.py
@@ -458,7 +458,7 @@
                         before = lon_speed(rows - 1, chunk, lo, lon[1])
                         flux_west = upwind(before, sp[rows - 2, lo:hi, s : s + w], own)
                         flux = upwind(lon_speed(rows, chunk, lo, lon[2]), own, unpack(plan_neg, chunk, recv_s.at[p, 1]))
-                    moved = own - (flux - flux_west) - lat_part(slots[2 + q], r, chunk, lo, own, lat[q], p == 0, p == tiles - 1, True)
+                    moved = own - (flux - flux_west) - lat_part(slots[2 + q], r, chunk, lo, own, lat[q], p - 1 not in pieces, p + 1 not in pieces, True)
                     slots[2 + q].moved[c, lo:hi, 0:w] = moved
                     sums[q] = add_up(chunk, moved, *sums[q])
             return source(slots[2:4], (0, rows - 1), lo, sums)
@@ -612,38 +612,40 @@
         if firsts[n] >= pairs:
             wait_group(n + 1)
     halo_faces()
+    edge(inner)
     for g in range(tops):
         first_arrives(g)
-    edge(every)
     ends_of(range(tops))
-    for g in range(tops):
+    for g in range(1, tops - 1):
+        send_ends(g)
+    edge(outer)
+    for g in (0, tops - 1):
         send_ends(g)
     lax.fori_loop(cut, pairs, step(inner), 0)
 
     def back(r, count, chunk, lo, west_t, east_t):
         c, s, w = chunk
-        hi = lo + TILE
-        own = [tt[r + q, c, 8 + lo : 8 + hi, 0:w] for q in range(count)]
-        line = [west_t] + own + [east_t]
-        steps = [line[q + 1] - line[q] for q in range(count + 1)]
-        speeds = [cxs[r + q, c, lo:hi, 0:w] for q in range(count + 1)]
-        for q in range(count):
-            value = own[q] + jnp.maximum(speeds[q + 1], 0.0) * steps[q + 1]
-            value = value + jnp.minimum(speeds[q], 0.0) * steps[q]
-            value = value + jnp.maximum(cys[r + q, c, 8 + lo : 8 + hi, 0:w], 0.0) * (tt[r + q, c, 9 + lo : 9 + hi, 0:w] - own[q])
-            value = value + jnp.minimum(cys[r + q, c, 7 + lo : 7 + hi, 0:w], 0.0) * (own[q] - tt[r + q, c, 7 + lo : 7 + hi, 0:w])
-            done[r + q, lo:hi, s : s + w] = value
-
-    def back_pair(k, carry):
-        r = 1 + 2 * k
+        at = lambda first: pl.ds(lo + first, TILE)
+        here, step = west_t, tt[r, c, at(8), 0:w] - west_t
+        speed = cxs[r, c, at(0), 0:w]
+        for q in range(r, r + count):
+            here = tt[q, c, at(8), 0:w]
+            value = here + jnp.minimum(speed, 0.0) * step
+            step = (east_t if q == r + count - 1 else tt[q + 1, c, at(8), 0:w]) - here
+            speed = cxs[q + 1, c, at(0), 0:w]
+            value = value + jnp.maximum(speed, 0.0) * step
+            value = value + jnp.maximum(cys[q, c, at(8), 0:w], 0.0) * (tt[q, c, at(9), 0:w] - here)
+            value = value + jnp.minimum(cys[q, c, at(7), 0:w], 0.0) * (here - tt[q, c, at(7), 0:w])
+            done[q, at(0), s : s + w] = value
+
+    def back_tile(a, carry):
+        lo = pl.multiple_of(a * TILE, TILE)
         for chunk in chunks:
             c, _, w = chunk
-            for lo in range(0, cells, TILE):
-                near = [tt[r + d, c, 8 + lo : 8 + lo + TILE, 0:w] for d in (-1, 2)]
-                back(r, 2, chunk, lo, *near)
+            back(1, rows - 2, chunk, lo, tt[0, c, pl.ds(lo + 8, TILE), 0:w], tt[rows - 1, c, pl.ds(lo + 8, TILE), 0:w])
         return carry
 
-    lax.fori_loop(0, pairs, back_pair, 0)
+    lax.fori_loop(0, tiles, back_tile, 0)
     for g in range(tops):
         second_arrives(g)
         rows_of = slice(TILE * g, TILE * g + TILE)

time: 18.8 us -> 18.4 us (0.979)
  Pallas kernels: 16.6 us -> 16.2 us
    pallas_call x1, Pallas kernels: 16.6 us -> 16.2 us  [body(): pl.pallas_call(functools.partial(kernel, nx, ny, plan_pos, plan_neg), out...]
where the time goes in v2:
time: 18.4 us; the launch traced here: 18.3 us
  Pallas kernels  16.2 us (88%)
  local copies, waits for them, and re-layouts  2.09 us (11%)
    pallas_call x1, Pallas kernels, body(): pl.pallas_call(functools.partial(kernel, nx, ny, plan_pos, plan_neg), out...  16.2 us
    unnamed x1, local copies, waits for them, and re-layouts  2.09 us

profile of v2, /device:TPU:0, one launch (start us, length us, event | category | flops | bytes accessed | tf_op | source)
XLA Modules:
  0.0 18.3 jit_solution(16062174466301315485)
XLA Ops:
  0.0 16.2 %step.1 = f32[24,40,1080]{2,1,0:T(8,128)S(1)} custom-call(f32[24,40,1080]{2,1,0:T(8,128)} %spectrum.1, f32[24,40,1080]{2,1,0:T(8,128)} %adjoint.1, f32[24,40]{1,0:T(8,128)} %cx_h.1, f32[24,40]{1,0:T(8,128)} %cy_h.1, f32[24,40]{1,0:T(8,128)} %wx_h.1, f32[24,40]{1,0:T(8,128)} %wy_h.1, s32[24,40]{1,0:T(8,128)} %land_h.1, s32[24,40]{1,0:T(8,128)} %ice_h.1, ...), custom_call_target="tpu_custom_call" | custom-call | tf_op jit(solution)/shard_map/step/pallas_call | solution.py:711
  16.2 2.1 %copy.14 = f32[24,40,1080]{2,1,0:T(8,128)} copy(f32[24,40,1080]{2,1,0:T(8,128)S(1)} %step.1) | data formatting | bytes 8294400

commit v3 on v2

--- a/solution.py
+++ b/solution.py
@@ -590,7 +590,7 @@
                     part_c[d, c, r : r + 1, 0:w] = nil[:, 0:w]
                     adj_c[d, c, r : r + 1, 0:w] = nil[:, 0:w]
 
-    cut = pairs // 2 + 1
+    cut = pairs // 2
     every, outer, inner = list(range(tiles)), [0, tiles - 1], list(range(1, tiles - 1))
 
     def step(chosen):

time: 18.4 us -> 18.1 us (0.984)
  Pallas kernels: 16.2 us -> 15.9 us
    pallas_call x1, Pallas kernels: 16.2 us -> 15.9 us  [body(): pl.pallas_call(functools.partial(kernel, nx, ny, plan_pos, plan_neg), out...]
where the time goes in v3:
time: 18.1 us; the launch traced here: 18 us
  Pallas kernels  15.9 us (88%)
  local copies, waits for them, and re-layouts  2.09 us (12%)
    pallas_call x1, Pallas kernels, body(): pl.pallas_call(functools.partial(kernel, nx, ny, plan_pos, plan_neg), out...  15.9 us
    unnamed x1, local copies, waits for them, and re-layouts  2.09 us

profile of v3, /device:TPU:0, one launch (start us, length us, event | category | flops | bytes accessed | tf_op | source)
XLA Modules:
  0.0 18.0 jit_solution(15439075811686566809)
XLA Ops:
  0.0 15.9 %step.1 = f32[24,40,1080]{2,1,0:T(8,128)S(1)} custom-call(f32[24,40,1080]{2,1,0:T(8,128)} %spectrum.1, f32[24,40,1080]{2,1,0:T(8,128)} %adjoint.1, f32[24,40]{1,0:T(8,128)} %cx_h.1, f32[24,40]{1,0:T(8,128)} %cy_h.1, f32[24,40]{1,0:T(8,128)} %wx_h.1, f32[24,40]{1,0:T(8,128)} %wy_h.1, s32[24,40]{1,0:T(8,128)} %land_h.1, s32[24,40]{1,0:T(8,128)} %ice_h.1, ...), custom_call_target="tpu_custom_call" | custom-call | tf_op jit(solution)/shard_map/step/pallas_call | solution.py:711
  15.9 2.1 %copy.14 = f32[24,40,1080]{2,1,0:T(8,128)} copy(f32[24,40,1080]{2,1,0:T(8,128)S(1)} %step.1) | data formatting | bytes 8294400
